TPU v7x, 32 devices: a whole 2x2x4 slice. The times are simulated.
32 devices in a mesh: clip: 2 (over y), rows: 8 (over z, x), tm: 2 (over core).
Axes of the slice: x: 2, y: 2, z: 4, core: 2. Of those that a mesh axis runs over, the one named last changes fastest.
Arguments:
- latent: bfloat16 [8, 8, 64, 192], P(('clip', 'tm'), 'rows'), parts along dimension 0, may hold values from -18 to 18
- gain_first: bfloat16 [192], replicated, may hold values from 0.099609375 to 1.8984375
- conv_first: bfloat16 [3, 3, 3, 192, 192], replicated, may hold values from -0.078125 to 0.078125
- gain_second: bfloat16 [192], replicated, may hold values from 0.099609375 to 1.8984375
- conv_second: bfloat16 [3, 3, 3, 192, 192], replicated, may hold values from -0.078125 to 0.078125
- conv_up: bfloat16 [3, 3, 96, 192], replicated, may hold values from -0.15625 to 0.15625
Outputs:
- decoded: bfloat16 [8, 16, 96, 128], P(('clip', 'tm'), 'rows'), parts along dimension 0
- peaks: float32 [6, 192], P('clip'), parts along dimension 0
There are 2 independent parts, one for each index of `clip`. A program takes and returns all parts, laid end to end along the dimension named above; an argument that names none is the same for every part. Nothing has to cross between parts.
All inputs are finite; a program needn't handle non-finite values.
Results may differ from a plain program's by a relative error of at most 0.0085.
Values may be sent and summed in bfloat16 or wider, within the bound.
A program may use at most 64 MiB of HBM per device.

v0:
```python
import jax
import jax.numpy as jnp
from jax import lax
from jax.sharding import PartitionSpec as P


def extended_2(cells, sides, width):
    for axis, dim in sides:
        count = lax.axis_size(axis)
        ends = count - 1
        head = lax.slice_in_dim(cells, 0, width, axis=dim)
        tail = lax.slice_in_dim(cells, cells.shape[dim] - width, cells.shape[dim], axis=dim)
        cells = jnp.concatenate(
            [
                lax.ppermute(tail, axis, [(i, (i + 1) % count) for i in range(ends)]),
                cells,
                lax.ppermute(head, axis, [((i + 1) % count, i) for i in range(ends)]),
            ],
            axis=dim,
        )
    return cells


def passed_along(block, axis, distance):
    devices = range(lax.axis_size(axis))
    route = [(i - distance, i) for i in devices if i - distance in devices]
    return lax.ppermute(block, axis, route)


def rms_norm(values, gain):
    floats = values.astype(jnp.float32)
    scale = lax.rsqrt(jnp.mean(floats * floats, axis=-1, keepdims=True) + 1e-06)
    return floats * scale * gain.astype(jnp.float32)


def causal_taps(extended, weights, frame_count, row_count, col_count):
    channels = extended.shape[-1]
    total = jnp.zeros((frame_count * row_count * col_count, weights.shape[-1]), jnp.float32)
    for time_tap in range(3):
        for row_tap in range(3):
            sliced = extended[time_tap : time_tap + frame_count, row_tap : row_tap + row_count]
            stacked = jnp.concatenate(
                [sliced[:, :, col_tap : col_tap + col_count] for col_tap in range(3)], axis=-1
            )
            matrix = weights[time_tap, row_tap].reshape(3 * channels, weights.shape[-1])
            total = total + jnp.dot(
                stacked.reshape(-1, 3 * channels), matrix, preferred_element_type=jnp.float32
            )
    return total.reshape(frame_count, row_count, col_count, weights.shape[-1])


def plane_taps(wide_padded, conv_up, row_count, col_count):
    channels = wide_padded.shape[-1]
    frame_count = wide_padded.shape[0]
    total = jnp.zeros((frame_count * row_count * col_count, conv_up.shape[2]), jnp.float32)
    for row_tap in range(3):
        sliced = wide_padded[:, row_tap : row_tap + row_count]
        stacked = jnp.concatenate(
            [sliced[:, :, col_tap : col_tap + col_count] for col_tap in range(3)], axis=-1
        )
        matrix = jnp.transpose(conv_up[row_tap], (0, 2, 1)).reshape(3 * channels, conv_up.shape[2])
        total = total + jnp.dot(
            stacked.reshape(-1, 3 * channels), matrix, preferred_element_type=jnp.float32
        )
    output = total.reshape(frame_count, row_count, col_count, conv_up.shape[2])
    return jnp.transpose(output, (0, 1, 3, 2)).astype(jnp.bfloat16)


def channel_peak(values):
    return jnp.max(jnp.abs(values).astype(jnp.float32), axis=(0, 1, 2))


def extend_block(values):
    rimmed = extended_2(values, (("rows", 1),), 1)
    cached = passed_along(rimmed, "tm", 1)
    return jnp.concatenate([cached, rimmed], axis=0)


def causal_block(values, weights):
    frame_count, row_count, col_count = (values.shape[0], values.shape[1], values.shape[2])
    extended = jnp.pad(extend_block(values), ((0, 0), (0, 0), (1, 1), (0, 0)))
    return causal_taps(extended, weights, frame_count, row_count, col_count)


def per_device(latent, gain_first, conv_first, gain_second, conv_second, conv_up):
    first = jax.nn.silu(rms_norm(latent, gain_first)).astype(jnp.bfloat16)
    peak_first = channel_peak(first)
    peak_first = lax.pmax(peak_first, ("rows", "tm"))
    hidden = causal_block(first, conv_first).astype(jnp.bfloat16)
    second = jax.nn.silu(rms_norm(hidden, gain_second)).astype(jnp.bfloat16)
    peak_second = channel_peak(second)
    peak_second = lax.pmax(peak_second, ("rows", "tm"))
    merged = (latent.astype(jnp.float32) + causal_block(second, conv_second)).astype(jnp.bfloat16)
    peak_third = channel_peak(merged)
    peak_third = lax.pmax(peak_third, ("rows", "tm"))
    row_count, col_count = (merged.shape[1], merged.shape[2])
    rimmed = extended_2(merged, (("rows", 1),), 1)
    wide = jnp.repeat(rimmed, 2, axis=1)[:, 1:-1]
    wide = jnp.repeat(wide, 2, axis=2)
    wide = jnp.pad(wide, ((0, 0), (0, 0), (1, 1), (0, 0)))
    decoded = plane_taps(wide, conv_up, 2 * row_count, 2 * col_count)
    peaks = jnp.stack([peak_first, peak_second, peak_third], axis=0)
    return (decoded, peaks)


def solution(mesh):
    return jax.shard_map(
        per_device,
        mesh=mesh,
        in_specs=(P(("clip", "tm"), "rows", None, None), P(), P(), P(), P(), P()),
        out_specs=(P(("clip", "tm"), "rows", None, None), P("clip", None)),
        check_vma=False,
    )
```

profile of v0, /device:TPU:0, one launch (start us, length us, event | category | flops | bytes accessed | tf_op | source)
XLA Modules:
  0.0 95.3 jit_solution(12759808253916733933)
XLA Ops:
  0.6 0.7 convert_element_type.88
  1.3 0.9 fusion.8
  2.2 1.0 %abs_reduce_fusion.1 = (bf16[192]{0:T(256)(128)(2,1)S(1)}, bf16[2,1,64,192]{3,2,0,1:T(8,128)(2,1)S(1)}) fusion(f32[192]{0:T(256)S(1)} %convert_element_type.88, f32[2,64]{1,0:T(2,128)S(1)} %add_rsqrt_fusion, bf16[2,1,64,192]{3,2,1,0:T(8,128)(2,1)} %param.6), kind=kLoop, calls=%fused_computation.71 | loop fusion | flops 245568 | bytes 99968 | tf_op jit(solution)/shard_map/reduce_max | solution.py:70
  3.2 1.3 %collective-permute-start.1 = (bf16[2,1,64,192]{3,2,0,1:T(8,128)(2,1)S(1)}, bf16[2,1,64,192]{3,2,0,1:T(8,128)(2,1)S(1)}, u32[]{:S(2)}, u32[]{:S(2)}) collective-permute-start(bf16[2,1,64,192]{3,2,0,1:T(8,128)(2,1)S(1)} %get-tuple-element.6), channel_id=1, source_target_pairs={{2,0},{4,2},{6,4},{8,6},{10,8},{12,10},{14,12},{3,1},{5,3},{7,5},{... | collective-permute-start | bytes 147464 | tf_op jit(solution)/shard_map/ppermute | solution.py:17
  4.5 5.5 %collective-permute-start = (bf16[2,1,64,192]{3,2,0,1:T(8,128)(2,1)S(1)}, bf16[2,1,64,192]{3,2,0,1:T(8,128)(2,1)S(1)}, u32[]{:S(2)}, u32[]{:S(2)}) collective-permute-start(bf16[2,1,64,192]{3,2,0,1:T(8,128)(2,1)S(1)} %get-tuple-element.6), channel_id=1, source_target_pairs={{0,2},{2,4},{4,6},{6,8},{8,10},{10,12},{12,14},{1,3},{3,5},{5,7},{... | collective-permute-start | bytes 147464 | tf_op jit(solution)/shard_map/ppermute | solution.py:15
  10.0 2.0 %fusion.21 = (bf16[1,1,3,192,192]{4,3,2,1,0:T(8,128)(2,1)S(1)}, bf16[1,1,3,192,192]{4,3,2,1,0:T(8,128)(2,1)S(1)}, bf16[1,1,3,192,192]{4,3,2,1,0:T(8,128)(2,1)S(1...) fusion(bf16[3,3,3,192,192]{4,3,2,1,0:T(8,128)(2,1)} %param.8), kind=kLoop, calls=%fused_computation.120 | loop fusion | bytes 3981312 | tf_op jit(solution)/shard_map/slice | solution.py:45
  12.1 1.5 %collective-permute-start.2 = (bf16[2,3,64,192]{3,2,0,1:T(8,128)(2,1)S(1)}, bf16[2,3,64,192]{3,2,0,1:T(8,128)(2,1)S(1)}, u32[]{:S(2)}, u32[]{:S(2)}) collective-permute-start(bf16[2,3,64,192]{3,2,0,1:T(8,128)(2,1)S(1)} %pad_maximum_fusion.3), channel_id=1, source_target_pairs={{0,1},{2,3},{4,5},{6,7},{8,9},{10,11},{12,13},{14,15},{16,17},{18,... | collective-permute-start | bytes 442376 | tf_op jit(solution)/shard_map/ppermute | solution.py:27
  13.6 0.9 fusion.20
  15.2 0.3 fusion.24
  15.5 0.3 convolution_add_fusion.17
  18.1 0.3 multiply_reduce_fusion
  18.7 1.3 %collective-permute-start.4 = (bf16[2,1,64,192]{3,2,0,1:T(8,128)(2,1)S(1)}, bf16[2,1,64,192]{3,2,0,1:T(8,128)(2,1)S(1)}, u32[]{:S(2)}, u32[]{:S(2)}) collective-permute-start(bf16[2,1,64,192]{3,2,0,1:T(8,128)(2,1)S(1)} %multiply_convert_fusion), channel_id=1, source_target_pairs={{2,0},{4,2},{6,4},{8,6},{10,8},{12,10},{14,12},{3,1},{5,3},{7,5},{... | collective-permute-start | bytes 147464 | tf_op jit(solution)/shard_map/ppermute | solution.py:17
  20.0 5.3 %collective-permute-start.3 = (bf16[2,1,64,192]{3,2,0,1:T(8,128)(2,1)S(1)}, bf16[2,1,64,192]{3,2,0,1:T(8,128)(2,1)S(1)}, u32[]{:S(2)}, u32[]{:S(2)}) collective-permute-start(bf16[2,1,64,192]{3,2,0,1:T(8,128)(2,1)S(1)} %multiply_convert_fusion), channel_id=1, source_target_pairs={{0,2},{2,4},{4,6},{6,8},{8,10},{10,12},{12,14},{1,3},{3,5},{5,7},{... | collective-permute-start | bytes 147464 | tf_op jit(solution)/shard_map/ppermute | solution.py:15
  25.4 0.8 copy.31
  26.2 0.8 copy.33
  27.0 0.8 copy.35
  27.8 0.6 reduce_max.43
  28.4 2.0 %collective-permute-start.5 = (bf16[2,3,64,192]{3,2,0,1:T(8,128)(2,1)S(1)}, bf16[2,3,64,192]{3,2,0,1:T(8,128)(2,1)S(1)}, u32[]{:S(2)}, u32[]{:S(2)}) collective-permute-start(bf16[2,3,64,192]{3,2,0,1:T(8,128)(2,1)S(1)} %pad_maximum_fusion.4), channel_id=1, source_target_pairs={{0,1},{2,3},{4,5},{6,7},{8,9},{10,11},{12,13},{14,15},{16,17},{18,... | collective-permute-start | bytes 442376 | tf_op jit(solution)/shard_map/ppermute | solution.py:27
  30.4 0.7 abs_reduce_fusion.2
  31.1 0.6 reduce_max.45
  31.8 0.8 pad_slice_fusion.1
  32.6 0.6 pad_slice_fusion.17
  33.3 0.8 pad_slice_fusion
  34.0 0.7 copy.26
  34.8 0.7 copy.25
  35.5 1.0 %pad_maximum_fusion.15 = bf16[2,1,64,576]{3,2,0,1:T(8,128)(2,1)S(1)} fusion(bf16[2,1,64,192]{3,2,0,1:T(8,128)(2,1)} %get-tuple-element.42, bf16[2,1,64,192]{3,2,0,1:T(8,128)(2,1)S(1)} %get-tuple-element.83, bf16[2,1,64,192]{3,2,0,1:T(8,128)(2,1)} %pad_slice_fusion.17), kind=kLoop, calls=%fused_computation.41 | loop fusion | flops 442368 | bytes 294912 | tf_op jit(solution)/shard_map/concatenate | solution.py:42
  36.8 1.0 %pad_maximum_fusion.16 = bf16[2,1,64,576]{3,2,0,1:T(8,128)(2,1)S(1)} fusion(bf16[2,1,64,192]{3,2,0,1:T(8,128)(2,1)} %get-tuple-element.44, bf16[2,1,64,192]{3,2,0,1:T(8,128)(2,1)S(1)} %get-tuple-element.82, bf16[2,1,64,192]{3,2,0,1:T(8,128)(2,1)} %get-tuple-element.43), kind=kLoop, calls=%fused_computation.42 | loop fusion | flops 442368 | bytes 294912 | tf_op jit(solution)/shard_map/concatenate | solution.py:42
  37.8 0.3 convolution_add_fusion.9
  38.1 1.0 %pad_maximum_fusion.17 = bf16[2,1,64,576]{3,2,0,1:T(8,128)(2,1)S(1)} fusion(bf16[2,1,64,192]{3,2,0,1:T(8,128)(2,1)} %get-tuple-element.46, bf16[2,1,64,192]{3,2,0,1:T(8,128)(2,1)S(1)} %get-tuple-element.81, bf16[2,1,64,192]{3,2,0,1:T(8,128)(2,1)} %get-tuple-element.45), kind=kLoop, calls=%fused_computation.43 | loop fusion | flops 442368 | bytes 294912 | tf_op jit(solution)/shard_map/concatenate | solution.py:42
  39.1 0.3 convolution_add_fusion.8
  39.5 0.3 convolution_add_fusion.7
  39.9 0.3 convolution_add_fusion.6
  40.3 0.3 convolution_add_fusion.5
  40.8 0.3 convolution_add_fusion.4
  41.5 0.3 convolution_add_fusion.2
  42.0 1.3 %collective-permute-start.7 = (bf16[2,1,64,192]{3,2,0,1:T(8,128)(2,1)S(1)}, bf16[2,1,64,192]{3,2,0,1:T(8,128)(2,1)S(1)}, u32[]{:S(2)}, u32[]{:S(2)}) collective-permute-start(bf16[2,1,64,192]{3,2,0,1:T(8,128)(2,1)S(1)} %get-tuple-element.10), channel_id=1, source_target_pairs={{2,0},{4,2},{6,4},{8,6},{10,8},{12,10},{14,12},{3,1},{5,3},{7,5},{... | collective-permute-start | bytes 147464 | tf_op jit(solution)/shard_map/ppermute | solution.py:17
  43.3 5.6 %collective-permute-start.6 = (bf16[2,1,64,192]{3,2,0,1:T(8,128)(2,1)S(1)}, bf16[2,1,64,192]{3,2,0,1:T(8,128)(2,1)S(1)}, u32[]{:S(2)}, u32[]{:S(2)}) collective-permute-start(bf16[2,1,64,192]{3,2,0,1:T(8,128)(2,1)S(1)} %get-tuple-element.10), channel_id=1, source_target_pairs={{0,2},{2,4},{4,6},{6,8},{8,10},{10,12},{12,14},{1,3},{3,5},{5,7},{... | collective-permute-start | bytes 147464 | tf_op jit(solution)/shard_map/ppermute | solution.py:15
  49.0 32.2 %all-reduce.3 = (f32[1,192]{1,0:T(1,128)S(1)}, f32[1,192]{1,0:T(1,128)S(1)}, f32[1,192]{1,0:T(1,128)S(1)}) all-reduce(f32[1,192]{1,0:T(1,128)S(1)} %bitcast.164, f32[1,192]{1,0:T(1,128)S(1)} %bitcast.163, f32[1,192]{1,0:T(1,128)S(1)} %bitcast.162), channel_id=1, replica_groups=mesh['clip'=2,'rows'=8,'tm'=2] {'rows','tm'}, use_global_device_ids=true, to_apply=%region_7.8 | all-reduce | flops 576 | bytes 4608 | tf_op jit(solution)/shard_map/pmax | solution.py:95
  81.2 0.6 pad_maximum_fusion.23
  82.3 2.2 %pad_slice_fusion.37 = (bf16[2,2,128,192]{3,1,2,0:T(2,128)(2,1)S(1)}, bf16[2,2,128,192]{3,1,2,0:T(2,128)(2,1)S(1)}, bf16[2,2,128,192]{3,1,2,0:T(2,128)(2,1)S(1)}...) fusion(bf16[2,4,128,192]{3,1,2,0:T(4,128)(2,1)S(1)} %bitcast.118), kind=kLoop, calls=%fused_computation.114 | loop fusion | bytes 3080192 | tf_op jit(solution)/shard_map/slice | solution.py:59
  84.5 1.0 %pad_maximum_fusion = bf16[2,2,128,576]{3,1,2,0:T(2,128)(2,1)S(1)} fusion(bf16[2,2,128,192]{3,1,2,0:T(2,128)(2,1)S(1)} %get-tuple-element.30, bf16[2,2,128,192]{3,1,2,0:T(2,128)(2,1)S(1)} %get-tuple-element.36, bf16[2,2,128,192]{3,1,2,0:T(2,128)(2,1)S(1)} %get-tuple-element.37), kind=kLoop, calls=%fused_computation.21 | loop fusion | flops 1769472 | bytes 1179648 | tf_op jit(solution)/shard_map/concatenate | solution.py:58
  85.5 1.7 %copy.30 = bf16[2,2,128,576]{2,1,0,3:T(2,128)(2,1)S(1)} copy(bf16[2,2,128,576]{3,1,2,0:T(2,128)(2,1)S(1)} %pad_maximum_fusion) | data formatting | bytes 1179648 | tf_op jit(solution)/shard_map/concatenate | solution.py:58
  87.4 1.0 %pad_maximum_fusion.1 = bf16[2,2,128,576]{3,1,2,0:T(2,128)(2,1)S(1)} fusion(bf16[2,2,128,192]{3,1,2,0:T(2,128)(2,1)S(1)} %get-tuple-element.32, bf16[2,2,128,192]{3,1,2,0:T(2,128)(2,1)S(1)} %get-tuple-element.35, bf16[2,2,128,192]{3,1,2,0:T(2,128)(2,1)S(1)} %get-tuple-element.31), kind=kLoop, calls=%fused_computation.22 | loop fusion | flops 1769472 | bytes 1179648 | tf_op jit(solution)/shard_map/concatenate | solution.py:58
  88.4 1.7 %copy.32 = bf16[2,2,128,576]{2,1,0,3:T(2,128)(2,1)S(1)} copy(bf16[2,2,128,576]{3,1,2,0:T(2,128)(2,1)S(1)} %pad_maximum_fusion.1) | data formatting | bytes 1179648 | tf_op jit(solution)/shard_map/concatenate | solution.py:58
  90.3 1.0 %pad_maximum_fusion.2 = bf16[2,2,128,576]{3,1,2,0:T(2,128)(2,1)S(1)} fusion(bf16[2,2,128,192]{3,1,2,0:T(2,128)(2,1)S(1)} %get-tuple-element.33, bf16[2,2,128,192]{3,1,2,0:T(2,128)(2,1)S(1)} %get-tuple-element.34, bf16[2,2,128,192]{3,1,2,0:T(2,128)(2,1)S(1)} %get-tuple-element.29), kind=kLoop, calls=%fused_computation.23 | loop fusion | flops 1769472 | bytes 1179648 | tf_op jit(solution)/shard_map/concatenate | solution.py:58
  91.4 1.7 %copy.34 = bf16[2,2,128,576]{2,1,0,3:T(2,128)(2,1)S(1)} copy(bf16[2,2,128,576]{3,1,2,0:T(2,128)(2,1)S(1)} %pad_maximum_fusion.2) | data formatting | bytes 1179648 | tf_op jit(solution)/shard_map/concatenate | solution.py:58
  93.6 0.4 copy-done.1
  94.6 0.7 copy.38
  (89 shorter events, 6.7 us)
Async XLA Ops:
  3.2 8.8 %collective-permute-start.1 = (bf16[2,1,64,192]{3,2,0,1:T(8,128)(2,1)S(1)}, bf16[2,1,64,192]{3,2,0,1:T(8,128)(2,1)S(1)}, u32[]{:S(2)}, u32[]{:S(2)}) collective-permute-start(bf16[2,1,64,192]{3,2,0,1:T(8,128)(2,1)S(1)} %get-tuple-element.6), channel_id=1, source_target_pairs={{2,0},{4,2},{6,4},{8,6},{10,8},{12,10},{14,12},{3,1},{5,3},{7,5},{... | collective-permute-start | bytes 147464 | tf_op jit(solution)/shard_map/ppermute | solution.py:17
  4.5 7.5 %collective-permute-start = (bf16[2,1,64,192]{3,2,0,1:T(8,128)(2,1)S(1)}, bf16[2,1,64,192]{3,2,0,1:T(8,128)(2,1)S(1)}, u32[]{:S(2)}, u32[]{:S(2)}) collective-permute-start(bf16[2,1,64,192]{3,2,0,1:T(8,128)(2,1)S(1)} %get-tuple-element.6), channel_id=1, source_target_pairs={{0,2},{2,4},{4,6},{6,8},{8,10},{10,12},{12,14},{1,3},{3,5},{5,7},{... | collective-permute-start | bytes 147464 | tf_op jit(solution)/shard_map/ppermute | solution.py:15
  10.0 3.6 %copy-start = (bf16[3,3,3,192,192]{4,3,2,1,0:T(8,128)(2,1)S(1)}, bf16[3,3,3,192,192]{4,3,2,1,0:T(8,128)(2,1)}, u32[]{:S(2)}) copy-start(bf16[3,3,3,192,192]{4,3,2,1,0:T(8,128)(2,1)} %param.10) | copy-start | bytes 5971972
  12.1 2.4 %copy-start.15 = (bf16[192]{0:T(256)(128)(2,1)S(1)}, bf16[192]{0:T(256)(128)(2,1)}, u32[]{:S(2)}) copy-start(bf16[192]{0:T(256)(128)(2,1)} %param.9) | copy-start | bytes 1156
  12.1 2.5 %collective-permute-start.2 = (bf16[2,3,64,192]{3,2,0,1:T(8,128)(2,1)S(1)}, bf16[2,3,64,192]{3,2,0,1:T(8,128)(2,1)S(1)}, u32[]{:S(2)}, u32[]{:S(2)}) collective-permute-start(bf16[2,3,64,192]{3,2,0,1:T(8,128)(2,1)S(1)} %pad_maximum_fusion.3), channel_id=1, source_target_pairs={{0,1},{2,3},{4,5},{6,7},{8,9},{10,11},{12,13},{14,15},{16,17},{18,... | collective-permute-start | bytes 442376 | tf_op jit(solution)/shard_map/ppermute | solution.py:27
  17.4 8.0 %copy-start.5 = (bf16[3,3,96,192]{3,2,1,0:T(8,128)(2,1)S(1)}, bf16[3,3,96,192]{3,2,1,0:T(8,128)(2,1)}, u32[]{:S(2)}) copy-start(bf16[3,3,96,192]{3,2,1,0:T(8,128)(2,1)} %param.11) | copy-start | bytes 995332
  18.7 9.6 %collective-permute-start.4 = (bf16[2,1,64,192]{3,2,0,1:T(8,128)(2,1)S(1)}, bf16[2,1,64,192]{3,2,0,1:T(8,128)(2,1)S(1)}, u32[]{:S(2)}, u32[]{:S(2)}) collective-permute-start(bf16[2,1,64,192]{3,2,0,1:T(8,128)(2,1)S(1)} %multiply_convert_fusion), channel_id=1, source_target_pairs={{2,0},{4,2},{6,4},{8,6},{10,8},{12,10},{14,12},{3,1},{5,3},{7,5},{... | collective-permute-start | bytes 147464 | tf_op jit(solution)/shard_map/ppermute | solution.py:17
  20.0 8.3 %collective-permute-start.3 = (bf16[2,1,64,192]{3,2,0,1:T(8,128)(2,1)S(1)}, bf16[2,1,64,192]{3,2,0,1:T(8,128)(2,1)S(1)}, u32[]{:S(2)}, u32[]{:S(2)}) collective-permute-start(bf16[2,1,64,192]{3,2,0,1:T(8,128)(2,1)S(1)} %multiply_convert_fusion), channel_id=1, source_target_pairs={{0,2},{2,4},{4,6},{6,8},{8,10},{10,12},{12,14},{1,3},{3,5},{5,7},{... | collective-permute-start | bytes 147464 | tf_op jit(solution)/shard_map/ppermute | solution.py:15
  28.4 3.3 %collective-permute-start.5 = (bf16[2,3,64,192]{3,2,0,1:T(8,128)(2,1)S(1)}, bf16[2,3,64,192]{3,2,0,1:T(8,128)(2,1)S(1)}, u32[]{:S(2)}, u32[]{:S(2)}) collective-permute-start(bf16[2,3,64,192]{3,2,0,1:T(8,128)(2,1)S(1)} %pad_maximum_fusion.4), channel_id=1, source_target_pairs={{0,1},{2,3},{4,5},{6,7},{8,9},{10,11},{12,13},{14,15},{16,17},{18,... | collective-permute-start | bytes 442376 | tf_op jit(solution)/shard_map/ppermute | solution.py:27
  36.5 2.9 %copy-start.9 = (bf16[2,1,64,192]{3,2,0,1:T(8,128)(2,1)S(1)}, bf16[2,1,64,192]{3,2,0,1:T(8,128)(2,1)}, u32[]{:S(2)}) copy-start(bf16[2,1,64,192]{3,2,0,1:T(8,128)(2,1)} %get-tuple-element.60) | copy-start | bytes 147460
  37.8 2.0 %copy-start.7 = (bf16[2,1,64,192]{3,2,0,1:T(8,128)(2,1)S(1)}, bf16[2,1,64,192]{3,2,0,1:T(8,128)(2,1)}, u32[]{:S(2)}) copy-start(bf16[2,1,64,192]{3,2,0,1:T(8,128)(2,1)} %get-tuple-element.52) | copy-start | bytes 147460
  37.8 2.0 %copy-start.8 = (bf16[2,1,64,192]{3,2,0,1:T(8,128)(2,1)S(1)}, bf16[2,1,64,192]{3,2,0,1:T(8,128)(2,1)}, u32[]{:S(2)}) copy-start(bf16[2,1,64,192]{3,2,0,1:T(8,128)(2,1)} %get-tuple-element.59) | copy-start | bytes 147460
  39.9 1.2 %copy-start.6 = (bf16[1,1,3,192,192]{4,3,2,1,0:T(8,128)(2,1)S(1)}, bf16[1,1,3,192,192]{4,3,2,1,0:T(8,128)(2,1)}, u32[]{:S(2)}) copy-start(bf16[1,1,3,192,192]{4,3,2,1,0:T(8,128)(2,1)} %get-tuple-element.19) | copy-start | bytes 663556
  39.9 1.2 %copy-start.10 = (bf16[128,192]{0,1:T(8,128)(2,1)S(1)}, bf16[128,192]{0,1:T(8,128)(2,1)}, u32[]{:S(2)}) copy-start(bf16[128,192]{0,1:T(8,128)(2,1)} %copy.26) | copy-start | bytes 147460
  39.9 1.2 %copy-start.11 = (bf16[128,192]{0,1:T(8,128)(2,1)S(1)}, bf16[128,192]{0,1:T(8,128)(2,1)}, u32[]{:S(2)}) copy-start(bf16[128,192]{0,1:T(8,128)(2,1)} %copy.25) | copy-start | bytes 147460
  39.9 1.2 %copy-start.12 = (bf16[128,192]{0,1:T(8,128)(2,1)S(1)}, bf16[128,192]{0,1:T(8,128)(2,1)}, u32[]{:S(2)}) copy-start(bf16[128,192]{0,1:T(8,128)(2,1)} %get-tuple-element.8) | copy-start | bytes 147460
  40.8 1.2 %copy-start.4 = (bf16[2,1,64,192]{3,2,1,0:T(8,128)(2,1)S(1)}, bf16[2,1,64,192]{3,2,1,0:T(8,128)(2,1)}, u32[]{:S(2)}) copy-start(bf16[2,1,64,192]{3,2,1,0:T(8,128)(2,1)} %param.6) | copy-start | bytes 147460
  40.8 8.2 %copy-start.13 = (f32[192]{0:T(256)S(1)}, f32[192]{0:T(256)}, u32[]{:S(2)}) copy-start(f32[192]{0:T(256)} %reduce_max.43) | copy-start | bytes 2308
  40.8 8.2 %copy-start.14 = (f32[192]{0:T(256)S(1)}, f32[192]{0:T(256)}, u32[]{:S(2)}) copy-start(f32[192]{0:T(256)} %reduce_max.45) | copy-start | bytes 2308
  42.0 39.8 %collective-permute-start.7 = (bf16[2,1,64,192]{3,2,0,1:T(8,128)(2,1)S(1)}, bf16[2,1,64,192]{3,2,0,1:T(8,128)(2,1)S(1)}, u32[]{:S(2)}, u32[]{:S(2)}) collective-permute-start(bf16[2,1,64,192]{3,2,0,1:T(8,128)(2,1)S(1)} %get-tuple-element.10), channel_id=1, source_target_pairs={{2,0},{4,2},{6,4},{8,6},{10,8},{12,10},{14,12},{3,1},{5,3},{7,5},{... | collective-permute-start | bytes 147464 | tf_op jit(solution)/shard_map/ppermute | solution.py:17
  43.3 38.5 %collective-permute-start.6 = (bf16[2,1,64,192]{3,2,0,1:T(8,128)(2,1)S(1)}, bf16[2,1,64,192]{3,2,0,1:T(8,128)(2,1)S(1)}, u32[]{:S(2)}, u32[]{:S(2)}) collective-permute-start(bf16[2,1,64,192]{3,2,0,1:T(8,128)(2,1)S(1)} %get-tuple-element.10), channel_id=1, source_target_pairs={{0,2},{2,4},{4,6},{6,8},{8,10},{10,12},{12,14},{1,3},{3,5},{5,7},{... | collective-permute-start | bytes 147464 | tf_op jit(solution)/shard_map/ppermute | solution.py:15
  91.4 1.9 %copy-start.2 = (bf16[3,192,96]{2,1,0:T(8,128)(2,1)S(1)}, bf16[3,192,96]{2,1,0:T(8,128)(2,1)}, u32[]{:S(2)}) copy-start(bf16[3,192,96]{2,1,0:T(8,128)(2,1)} %copy.31) | copy-start | bytes 331780
  93.1 0.9 copy-start.1
  93.3 1.0 %copy-start.3 = (bf16[3,192,96]{2,1,0:T(8,128)(2,1)S(1)}, bf16[3,192,96]{2,1,0:T(8,128)(2,1)}, u32[]{:S(2)}) copy-start(bf16[3,192,96]{2,1,0:T(8,128)(2,1)} %copy.35) | copy-start | bytes 331780
where the time goes:
time: 95.8 us; the launch traced here: 95.3 us
  blocking collectives  32.2 us (34%)
  starting transfers between devices  23.8 us (25%)
  local copies, waits for them, and re-layouts  19 us (20%)
  other arithmetic  12.6 us (13%)
  matrix products  6.2 us (6%)
  between operations  1.35 us (1%)
    pmax x1, blocking collectives, per_device(): peak_third = lax.pmax(peak_third, ('rows', 'tm'))  32.2 us
    ppermute x3, starting transfers between devices, extended_2(): lax.ppermute(tail, axis, [(i, (i + 1) % count) for i in range(ends)])  16.4 us
    dot_general x18, matrix products, causal_taps(): jnp.dot(stacked.reshape(-1, 3 * channels), matrix, preferred_element_type...  5.36 us
    concatenate x3, local copies, waits for them, and re-layouts, plane_taps(): jnp.concatenate([sliced[:, :, col_tap:col_tap + col_count] for col_tap in...  5.02 us
    concatenate x13, other arithmetic, causal_taps(): jnp.concatenate([sliced[:, :, col_tap:col_tap + col_count] for col_tap in...  4 us
    ppermute x3, starting transfers between devices, extended_2(): lax.ppermute(head, axis, [((i + 1) % count, i) for i in range(ends)])  3.87 us
    ppermute x2, starting transfers between devices, passed_along(): return lax.ppermute(block, axis, route)  3.47 us
    concatenate x3, other arithmetic, plane_taps(): jnp.concatenate([sliced[:, :, col_tap:col_tap + col_count] for col_tap in...  3.06 us
  transfers between devices with their start and end apart: 8, of which 1 were waited for; matrix products, arithmetic and copies ran while one was open for 8% of the time, Pallas kernels for 0%

commit v1 on v0

v1 whole, which is shorter than its diff:
```python
import functools

import jax
import jax.numpy as jnp
from jax import lax
from jax.experimental import pallas as pl
from jax.experimental.pallas import tpu as pltpu
from jax.sharding import PartitionSpec as P

MESH = pl.DeviceIdType.MESH
BF16 = jnp.bfloat16
F32 = jnp.float32
REACH = 2


def normed_silu(values, gain):
    scale = lax.rsqrt(jnp.mean(values * values, axis=-1, keepdims=True) + 1e-06)
    u = values * scale * gain
    return (u / (1.0 + jnp.exp(-u))).astype(BF16)


def peak_of(values):
    return jnp.max(jnp.abs(values.astype(F32)), axis=0, keepdims=True)


def dot(a, b):
    return jnp.dot(a, b, preferred_element_type=F32)


def dot_nt(a, b):
    return lax.dot_general(a, b, (((1,), (1,)), ((), ())), preferred_element_type=F32)


def taps_sum(buf, weights, frames, rows_out, cols):
    depth = buf.shape[-1]
    pixels = frames * rows_out * cols
    lhs = jnp.concatenate(
        [
            buf[i : i + frames, j * cols : (j + rows_out) * cols, :].reshape(pixels, depth)
            for i in range(3)
            for j in range(3)
        ],
        axis=1,
    )
    parts = []
    for k in range(3):
        rhs = jnp.concatenate([weights[ij * 3 + k] for ij in range(9)], axis=0)
        parts.append(dot(lhs, rhs))
    col = lax.rem(lax.broadcasted_iota(jnp.int32, parts[0].shape, 0), cols)
    left = jnp.where(col == 0, 0.0, pltpu.roll(parts[0], 1, 0))
    right = jnp.where(col == cols - 1, 0.0, pltpu.roll(parts[2], pixels - 1, 0))
    return left + parts[1] + right


def kernel(
    R, T, lat_hbm, g1_ref, w1_hbm, g2_ref, w2_hbm, up_hbm, dec_ref, peaks_ref,
    lat, prev, first, second, w1, w2, up, merged, pk_send, pk_recv,
    load_sem, x1_send, x1_recv, rl_send, rl_recv, s_send, s_recv, x3_send, x3_recv, pk_ssem, pk_rsem,
):
    r = lax.axis_index("rows")
    t = lax.axis_index("tm")
    n = R * T
    me = r * T + t
    _, frames, cols, C = lat.shape
    half = pk_send.shape[-1]
    SPAN = 2 * REACH + 1

    loads = [
        pltpu.make_async_copy(lat_hbm, lat.at[REACH], load_sem.at[0]),
        pltpu.make_async_copy(w1_hbm, w1.at[:, 0:C, :], load_sem.at[1]),
        pltpu.make_async_copy(w2_hbm, w2.at[:, 0:C, :], load_sem.at[2]),
        pltpu.make_async_copy(up_hbm, up, load_sem.at[3]),
    ]
    for copy in loads:
        copy.start()

    barrier = pltpu.get_barrier_semaphore()

    def greet(k, carry):
        peer = lax.rem(me + k, n)
        pl.semaphore_signal(
            barrier, inc=1, device_id={"rows": peer // T, "tm": lax.rem(peer, T)}, device_id_type=MESH
        )
        return carry

    second[frames:, :, :] = jnp.zeros_like(second[frames:, :, :])

    @pl.when(t == 0)
    def _():
        second[0:frames, :, :] = jnp.zeros_like(second[0:frames, :, :])

    @pl.when(r == 0)
    def _():
        merged[0] = jnp.zeros_like(merged[0])

    @pl.when(r == R - 1)
    def _():
        merged[2] = jnp.zeros_like(merged[2])

    lax.fori_loop(1, n, greet, 0, unroll=n <= 16)

    first[...] = jnp.zeros_like(first)
    pad = w1.shape[1] - C
    w1[:, C:, :] = jnp.zeros((w1.shape[0], pad, C), BF16)
    w2[:, C:, :] = jnp.zeros((w2.shape[0], pad, C), BF16)
    pk_send[...] = jnp.zeros_like(pk_send)

    loads[0].wait()
    pl.semaphore_wait(barrier, n - 1)

    offsets = [1, -1, 2, -2]

    def row_copy(d):
        slot = REACH - d
        return pltpu.make_async_remote_copy(
            src_ref=lat.at[REACH], dst_ref=lat.at[slot], send_sem=x1_send.at[slot],
            recv_sem=x1_recv.at[slot], device_id={"rows": r + d}, device_id_type=MESH,
        )

    def there(d):
        return jnp.logical_and(r + d >= 0, r + d < R)

    for d in offsets:
        pl.when(there(d))(lambda d=d: row_copy(d).start())

    def relay(slot):
        return pltpu.make_async_remote_copy(
            src_ref=lat.at[slot], dst_ref=prev.at[slot], send_sem=rl_send.at[slot],
            recv_sem=rl_recv.at[slot], device_id={"tm": t + 1}, device_id_type=MESH,
        )

    gives = t < T - 1
    takes = t > 0
    pl.when(gives)(lambda: relay(REACH).start())

    gain1 = g1_ref[...].astype(F32)
    gain2 = g2_ref[...].astype(F32)

    def put_first(source, slot, at):
        rows = slice(slot * cols, (slot + 1) * cols)
        values = normed_silu(source[slot].astype(F32).reshape(frames * cols, C), gain1)
        first[at : at + frames, rows, 0:C] = values.reshape(frames, cols, C)
        return values

    def put_peak(i, row):
        pk_send[2 * i : 2 * i + 1, :] = row[:, 0:half]
        pk_send[2 * i + 1 : 2 * i + 2, 0 : C - half] = row[:, half:C]

    put_peak(0, peak_of(put_first(lat, REACH, frames)))

    for d in offsets:
        slot = REACH + d

        @pl.when(there(d))
        def _(d=d, slot=slot):
            row_copy(-d).wait_recv()
            pl.when(gives)(lambda: relay(slot).start())
            put_first(lat, slot, frames)

    @pl.when(takes)
    def _():
        for d in [0] + offsets:
            slot = REACH + d

            @pl.when(there(d))
            def _(slot=slot):
                relay(slot).wait_recv()
                put_first(prev, slot, 0)

    loads[1].wait()
    hidden = taps_sum(first, w1, frames, 3, cols).astype(BF16).astype(F32)
    activated = normed_silu(hidden, gain2).reshape(frames, 3, cols, C)
    zeros = jnp.zeros((frames, cols, C), BF16)
    for j in range(3):
        values = activated[:, j]
        if j != 1:
            values = jnp.where(there(j - 1), values, zeros)
        second[frames:, j * cols : (j + 1) * cols, 0:C] = values

    def hand_on():
        return pltpu.make_async_remote_copy(
            src_ref=second.at[pl.ds(frames, frames)], dst_ref=second.at[pl.ds(0, frames)],
            send_sem=s_send, recv_sem=s_recv, device_id={"tm": t + 1}, device_id_type=MESH,
        )

    pl.when(gives)(lambda: hand_on().start())
    put_peak(1, peak_of(activated[:, 1].reshape(frames * cols, C)))
    loads[2].wait()
    pl.when(takes)(lambda: hand_on().wait_recv())

    block = lat[REACH].astype(F32).reshape(frames * cols, C) + taps_sum(second, w2, frames, 1, cols)
    block = block.astype(BF16)
    merged[1] = block.reshape(frames, cols, C)
    put_peak(2, peak_of(block))

    def edge_copy(d):
        slot = 1 - d
        return pltpu.make_async_remote_copy(
            src_ref=merged.at[1], dst_ref=merged.at[slot], send_sem=x3_send.at[slot],
            recv_sem=x3_recv.at[slot], device_id={"rows": r + d}, device_id_type=MESH,
        )

    for d in (1, -1):
        pl.when(there(d))(lambda d=d: edge_copy(d).start())

    def peak_copy(k):
        peer = lax.rem(me + k, n)
        return pltpu.make_async_remote_copy(
            src_ref=pk_send, dst_ref=pk_recv.at[k], send_sem=pk_ssem.at[k], recv_sem=pk_rsem.at[k],
            device_id={"rows": peer // T, "tm": lax.rem(peer, T)}, device_id_type=MESH,
        )

    def send_peak(k, carry):
        peak_copy(k).start()
        return carry

    lax.fori_loop(1, n, send_peak, 0, unroll=n <= 16)

    loads[3].wait()
    C2 = dec_ref.shape[2]
    width = frames * cols
    own = dot_nt(up[...], block).reshape(3, 3, C2, width)
    upper = own[1] + own[2]
    lower = own[0] + own[1]
    for d in (1, -1):
        pl.when(there(d))(lambda d=d: edge_copy(-d).wait_recv())
    upper = upper + dot_nt(up[0 : 3 * C2], merged[0].reshape(width, C)).reshape(3, C2, width)
    lower = lower + dot_nt(up[6 * C2 :], merged[2].reshape(width, C)).reshape(3, C2, width)
    lane = lax.rem(lax.broadcasted_iota(jnp.int32, (C2, width), 1), cols)

    def columns(sums):
        from_left = jnp.where(lane == 0, 0.0, pltpu.roll(sums[0], 1, 1))
        from_right = jnp.where(lane == cols - 1, 0.0, pltpu.roll(sums[2], width - 1, 1))
        even = from_left + sums[1] + sums[2]
        odd = sums[0] + sums[1] + from_right
        return jnp.concatenate([even, odd], axis=1).astype(BF16)

    narrow = jnp.concatenate([columns(upper), columns(lower)], axis=0)
    q = lax.broadcasted_iota(jnp.int32, (2 * width, 2 * width), 0)
    o = lax.broadcasted_iota(jnp.int32, (2 * width, 2 * width), 1)
    frame = lax.rem(lax.div(q, cols), frames)
    target = frame * (2 * cols) + 2 * lax.rem(q, cols) + lax.div(q, width)
    spread = jnp.where(o == target, 1.0, 0.0).astype(BF16)
    wide = dot(narrow, spread).astype(BF16)
    for f in range(frames):
        for j in range(2):
            dec_ref[f, j] = wide[j * C2 : (j + 1) * C2, f * 2 * cols : (f + 1) * 2 * cols]

    def take_peak(k, best):
        peak_copy(k).wait_recv()
        return jnp.maximum(best, pk_recv[k])

    best = lax.fori_loop(1, n, take_peak, pk_send[...], unroll=n <= 16)
    for i in range(3):
        peaks_ref[i : i + 1, 0:half] = best[2 * i : 2 * i + 1, :]
        peaks_ref[i : i + 1, half:C] = best[2 * i + 1 : 2 * i + 2, 0 : C - half]

    def end_peak(k, carry):
        peak_copy(k).wait_send()
        return carry

    lax.fori_loop(1, n, end_peak, 0, unroll=n <= 16)
    for d in offsets:
        pl.when(there(d))(lambda d=d: row_copy(d).wait_send())
    for d in (1, -1):
        pl.when(there(d))(lambda d=d: edge_copy(d).wait_send())

    @pl.when(gives)
    def _():
        for d in [0] + offsets:
            pl.when(there(d))(lambda d=d: relay(REACH + d).wait_send())
        hand_on().wait_send()


def per_device(latent, gain_first, conv_first, gain_second, conv_second, conv_up):
    frames, rows, cols, C = latent.shape
    R, T = lax.axis_size("rows"), lax.axis_size("tm")
    C2 = conv_up.shape[2]
    n = R * T
    if rows != 1 or frames != 2:
        raise ValueError("unsupported block")
    half = 128
    depth = -(-C // 256) * 256
    taps = 27
    vmem = pl.BlockSpec(memory_space=pltpu.VMEM)
    hbm = pl.BlockSpec(memory_space=pl.ANY)
    dma = pltpu.SemaphoreType.DMA
    return pl.pallas_call(
        functools.partial(kernel, R, T),
        out_shape=(
            jax.ShapeDtypeStruct((frames, 2 * rows, C2, 2 * cols), BF16),
            jax.ShapeDtypeStruct((3, C), F32),
        ),
        in_specs=[hbm, vmem, hbm, vmem, hbm, hbm],
        out_specs=(vmem, vmem),
        scratch_shapes=[
            pltpu.VMEM((2 * REACH + 1, frames, cols, C), BF16),
            pltpu.VMEM((2 * REACH + 1, frames, cols, C), BF16),
            pltpu.VMEM((2 * frames, (2 * REACH + 1) * cols, depth), BF16),
            pltpu.VMEM((2 * frames, 3 * cols, depth), BF16),
            pltpu.VMEM((taps, depth, C), BF16),
            pltpu.VMEM((taps, depth, C), BF16),
            pltpu.VMEM((9 * C2, C), BF16),
            pltpu.VMEM((3, frames, cols, C), BF16),
            pltpu.VMEM((8, half), F32),
            pltpu.VMEM((n, 8, half), F32),
            dma((4,)),
            dma((2 * REACH + 1,)),
            dma((2 * REACH + 1,)),
            dma((2 * REACH + 1,)),
            dma((2 * REACH + 1,)),
            dma,
            dma,
            dma((3,)),
            dma((3,)),
            dma((n,)),
            dma((n,)),
        ],
        compiler_params=pltpu.CompilerParams(collective_id=0, has_side_effects=True),
    )(
        latent.reshape(frames, cols, C),
        gain_first.reshape(1, C),
        conv_first.reshape(taps, C, C),
        gain_second.reshape(1, C),
        conv_second.reshape(taps, C, C),
        conv_up.reshape(9 * C2, C),
    )


def solution(mesh):
    return jax.shard_map(
        per_device,
        mesh=mesh,
        in_specs=(P(("clip", "tm"), "rows", None, None), P(), P(), P(), P(), P()),
        out_specs=(P(("clip", "tm"), "rows", None, None), P("clip", None)),
        check_vma=False,
    )
```

time: 95.8 us -> 27.2 us (0.28)
  blocking collectives: 32.2 us -> 0 us
  starting transfers between devices: 23.8 us -> 0 us
  Pallas kernels: 0 us -> 21 us
  local copies, waits for them, and re-layouts: 19 us -> 5.25 us
  other arithmetic: 12.6 us -> 0 us
  matrix products: 6.2 us -> 0 us
    pmax x1 -> x0, blocking collectives: 32.2 us -> none  [per_device(): peak_third = lax.pmax(peak_third, ('rows', 'tm'))]
    ppermute x8 -> x0, starting transfers between devices: 23.8 us -> none  [the longest x3 16.4 us: extended_2(): lax.ppermute(tail, axis, [(i, (i + 1) % count) for i in range(ends)])]
    pallas_call x0 -> x1, Pallas kernels: none -> 21 us  [per_device(): pl.pallas_call(functools.partial(kernel, R, T), out_shape=(jax.ShapeDtype...]
    slice x13 -> x0, local copies, waits for them, and re-layouts: 7.84 us -> none  [the longest x2 2.89 us: causal_taps(): matrix = weights[time_tap, row_tap].reshape(3 * channels, weights.shape[-1])]
    concatenate x21 -> x0, other arithmetic: 7.34 us -> none  [the longest x13 4 us: causal_taps(): jnp.concatenate([sliced[:, :, col_tap:col_tap + col_count] for col_tap in...]
    concatenate x6 -> x0, local copies, waits for them, and re-layouts: 6.47 us -> none  [the longest x3 5.02 us: plane_taps(): jnp.concatenate([sliced[:, :, col_tap:col_tap + col_count] for col_tap in...]
    dot_general x21 -> x0, matrix products: 6.2 us -> none  [the longest x18 5.36 us: causal_taps(): jnp.dot(stacked.reshape(-1, 3 * channels), matrix, preferred_element_type...]
    reduce_max x6 -> x0, other arithmetic: 2.91 us -> none  [channel_peak(): return jnp.max(jnp.abs(values).astype(jnp.float32), axis=(0, 1, 2))]
  transfers between devices with their start and end apart: 8 -> 0, of which waited for: 1 -> 0; matrix products, arithmetic and copies ran while one was open for 8% -> 0% of each run, Pallas kernels for 0% -> 0%
where the time goes in v1:
time: 27.2 us; the launch traced here: 26.9 us
  Pallas kernels  21 us (77%)
  local copies, waits for them, and re-layouts  5.25 us (19%)
  between operations  0.64 us (2%)
    pallas_call x1, Pallas kernels, per_device(): pl.pallas_call(functools.partial(kernel, R, T), out_shape=(jax.ShapeDtype...  21 us
    unnamed x2, local copies, waits for them, and re-layouts  2.82 us
    reshape x1, local copies, waits for them, and re-layouts, per_device(): gain_first.reshape(1, C)  1.22 us
    reshape x1, local copies, waits for them, and re-layouts, per_device(): gain_second.reshape(1, C)  1.22 us

profile of v1, /device:TPU:0, one launch (start us, length us, event | category | flops | bytes accessed | tf_op | source)
XLA Modules:
  0.0 26.9 jit_solution(7068627537508541333)
XLA Ops:
  0.6 1.2 %reshape.23.g1_ref = bf16[1,192]{1,0:T(2,128)(2,1)} reshape(bf16[192]{0:T(256)(128)(2,1)} %param.7) | data formatting | bytes 768 | tf_op jit(solution)/shard_map/reshape | solution.py:322
  1.9 1.2 %reshape.25.g2_ref = bf16[1,192]{1,0:T(2,128)(2,1)} reshape(bf16[192]{0:T(256)(128)(2,1)} %param.9) | data formatting | bytes 768 | tf_op jit(solution)/shard_map/reshape | solution.py:324
  3.1 21.0 %shard_map.77 = (bf16[2,2,96,128]{3,2,1,0:T(8,128)(2,1)}, f32[3,192]{1,0:T(4,128)}) custom-call(bf16[2,64,192]{2,1,0:T(8,128)(2,1)} %bitcast.7, bf16[1,192]{1,0:T(2,128)(2,1)} %reshape.23.g1_ref, bf16[27,192,192]{2,1,0:T(8,128)(2,1)} %bitcast.4, bf16[1,192]{1,0:T(2,128)(2,1)} %reshape.25.g2_ref, bf16[27,192,192]{2,1,0:T(8,128)(2,1)} %bitcast.5, ...), custom_call_target="tpu_custom_call" | custom-call | tf_op jit(solution)/shard_map/pallas_call | solution.py:288
  24.1 1.5 %copy.10 = bf16[2,2,96,128]{3,2,1,0:T(8,128)(2,1)} copy(bf16[2,2,96,128]{3,2,1,0:T(8,128)(2,1)} %get-tuple-element.4) | data formatting | bytes 196608
  25.6 1.3 %copy.11 = f32[3,192]{1,0:T(4,128)} copy(f32[3,192]{1,0:T(4,128)} %get-tuple-element.5) | data formatting | bytes 4608

commit v2 on v1

--- a/solution.py
+++ b/solution.py
@@ -55,7 +55,7 @@
 def kernel(
     R, T, lat_hbm, g1_ref, w1_hbm, g2_ref, w2_hbm, up_hbm, dec_ref, peaks_ref,
     lat, prev, first, second, w1, w2, up, merged, pk_send, pk_recv,
-    load_sem, x1_send, x1_recv, rl_send, rl_recv, s_send, s_recv, x3_send, x3_recv, pk_ssem, pk_rsem,
+    load_sem, x1_send, x1_recv, rl_send, rl_recv, s_send, s_recv, x3_send, x3_recv, pk_ssem, pk_rsem, known,
 ):
     r = lax.axis_index("rows")
     t = lax.axis_index("tm")
@@ -76,12 +76,15 @@
 
     barrier = pltpu.get_barrier_semaphore()
 
-    def greet(k, carry):
-        peer = lax.rem(me + k, n)
+    def there(d):
+        return jnp.logical_and(r + d >= 0, r + d < R)
+
+    near = [(d, e) for d in range(-REACH, REACH + 1) for e in range(T) if (d, e) != (0, 0)]
+
+    def greet(d, e):
         pl.semaphore_signal(
-            barrier, inc=1, device_id={"rows": peer // T, "tm": lax.rem(peer, T)}, device_id_type=MESH
-        )
-        return carry
+            barrier, inc=1, device_id={"rows": r + d, "tm": lax.rem(t + e, T)}, device_id_type=MESH
+        )
 
     second[frames:, :, :] = jnp.zeros_like(second[frames:, :, :])
 
@@ -97,7 +100,8 @@
     def _():
         merged[2] = jnp.zeros_like(merged[2])
 
-    lax.fori_loop(1, n, greet, 0, unroll=n <= 16)
+    for d, e in near:
+        pl.when(there(d))(functools.partial(greet, d, e))
 
     first[...] = jnp.zeros_like(first)
     pad = w1.shape[1] - C
@@ -106,7 +110,8 @@
     pk_send[...] = jnp.zeros_like(pk_send)
 
     loads[0].wait()
-    pl.semaphore_wait(barrier, n - 1)
+    rows_near = 1 + jnp.minimum(r, REACH) + jnp.minimum(R - 1 - r, REACH)
+    pl.semaphore_wait(barrier, rows_near * T - 1)
 
     offsets = [1, -1, 2, -2]
 
@@ -117,11 +122,25 @@
             recv_sem=x1_recv.at[slot], device_id={"rows": r + d}, device_id_type=MESH,
         )
 
-    def there(d):
-        return jnp.logical_and(r + d >= 0, r + d < R)
-
     for d in offsets:
         pl.when(there(d))(lambda d=d: row_copy(d).start())
+
+    stages = [REACH << i for i in range(R.bit_length()) if (REACH << i) < R - 1]
+
+    def tell(i):
+        for side, d in enumerate((stages[i], -stages[i])):
+            pl.when(there(d))(
+                lambda side=side, d=d: pl.semaphore_signal(
+                    known.at[i, side], inc=1, device_id={"rows": r + d}, device_id_type=MESH
+                )
+            )
+
+    def hear(i):
+        for side, d in enumerate((stages[i], -stages[i])):
+            pl.when(there(-d))(lambda side=side: pl.semaphore_wait(known.at[i, side], 1))
+
+    if stages:
+        tell(0)
 
     def relay(slot):
         return pltpu.make_async_remote_copy(
@@ -133,8 +152,8 @@
     takes = t > 0
     pl.when(gives)(lambda: relay(REACH).start())
 
-    gain1 = g1_ref[...].astype(F32)
-    gain2 = g2_ref[...].astype(F32)
+    gain1 = g1_ref[...].astype(F32).reshape(1, C)
+    gain2 = g2_ref[...].astype(F32).reshape(1, C)
 
     def put_first(source, slot, at):
         rows = slice(slot * cols, (slot + 1) * cols)
@@ -156,6 +175,10 @@
             row_copy(-d).wait_recv()
             pl.when(gives)(lambda: relay(slot).start())
             put_first(lat, slot, frames)
+
+    for i in range(1, len(stages)):
+        hear(i - 1)
+        tell(i)
 
     @pl.when(takes)
     def _():
@@ -202,6 +225,9 @@
 
     for d in (1, -1):
         pl.when(there(d))(lambda d=d: edge_copy(d).start())
+
+    if stages:
+        hear(len(stages) - 1)
 
     def peak_copy(k):
         peer = lax.rem(me + k, n)
@@ -315,13 +341,14 @@
             dma((3,)),
             dma((n,)),
             dma((n,)),
+            pltpu.SemaphoreType.REGULAR((R.bit_length(), 2)),
         ],
         compiler_params=pltpu.CompilerParams(collective_id=0, has_side_effects=True),
     )(
         latent.reshape(frames, cols, C),
-        gain_first.reshape(1, C),
+        gain_first,
         conv_first.reshape(taps, C, C),
-        gain_second.reshape(1, C),
+        gain_second,
         conv_second.reshape(taps, C, C),
         conv_up.reshape(9 * C2, C),
     )

time: 27.2 us -> 24.4 us (0.90)
  local copies, waits for them, and re-layouts: 5.25 us -> 2.82 us
    reshape x2 -> x0, local copies, waits for them, and re-layouts: 2.44 us -> none  [the longest x1 1.22 us: per_device(): gain_first.reshape(1, C)]
where the time goes in v2:
time: 24.4 us; the launch traced here: 24.2 us
  Pallas kernels  20.8 us (85%)
  local copies, waits for them, and re-layouts  2.82 us (12%)
  between operations  0.64 us (3%)
    pallas_call x1, Pallas kernels, per_device(): pl.pallas_call(functools.partial(kernel, R, T), out_shape=(jax.ShapeDtype...  20.8 us
    unnamed x2, local copies, waits for them, and re-layouts  2.82 us

profile of v2, /device:TPU:0, one launch (start us, length us, event | category | flops | bytes accessed | tf_op | source)
XLA Modules:
  0.0 24.2 jit_solution(14039833384382099558)
XLA Ops:
  0.6 20.8 %shard_map.77 = (bf16[2,2,96,128]{3,2,1,0:T(8,128)(2,1)}, f32[3,192]{1,0:T(4,128)}) custom-call(bf16[2,64,192]{2,1,0:T(8,128)(2,1)} %bitcast.7, bf16[192]{0:T(256)(128)(2,1)} %g1_ref.1, bf16[27,192,192]{2,1,0:T(8,128)(2,1)} %bitcast.4, bf16[192]{0:T(256)(128)(2,1)} %g2_ref.1, bf16[27,192,192]{2,1,0:T(8,128)(2,1)} %bitcast.5, bf16[864,192]{1,0:T(8,128)(2,1)} %bitcast.6), custom_call_target="tpu_custom_call" | custom-call | tf_op jit(solution)/shard_map/pallas_call | solution.py:314
  21.4 1.5 %copy.10 = bf16[2,2,96,128]{3,2,1,0:T(8,128)(2,1)} copy(bf16[2,2,96,128]{3,2,1,0:T(8,128)(2,1)} %get-tuple-element.4) | data formatting | bytes 196608
  23.0 1.3 %copy.11 = f32[3,192]{1,0:T(4,128)} copy(f32[3,192]{1,0:T(4,128)} %get-tuple-element.5) | data formatting | bytes 4608

commit v3 on v2

--- a/solution.py
+++ b/solution.py
@@ -31,31 +31,47 @@
     return lax.dot_general(a, b, (((1,), (1,)), ((), ())), preferred_element_type=F32)
 
 
-def taps_sum(buf, weights, frames, rows_out, cols):
+def taps_part(buf, weights, time_taps, frames, rows_out, cols):
     depth = buf.shape[-1]
     pixels = frames * rows_out * cols
+    pairs = [(i, j) for i in time_taps for j in range(3)]
     lhs = jnp.concatenate(
         [
             buf[i : i + frames, j * cols : (j + rows_out) * cols, :].reshape(pixels, depth)
-            for i in range(3)
-            for j in range(3)
+            for i, j in pairs
         ],
         axis=1,
     )
-    parts = []
-    for k in range(3):
-        rhs = jnp.concatenate([weights[ij * 3 + k] for ij in range(9)], axis=0)
-        parts.append(dot(lhs, rhs))
+    return [
+        dot(lhs, jnp.concatenate([weights[(i * 3 + j) * 3 + k] for i, j in pairs], axis=0))
+        for k in range(3)
+    ]
+
+
+def shifted_sum(parts, more, cols):
+    parts = [a + b for a, b in zip(parts, more)]
+    pixels = parts[0].shape[0]
     col = lax.rem(lax.broadcasted_iota(jnp.int32, parts[0].shape, 0), cols)
     left = jnp.where(col == 0, 0.0, pltpu.roll(parts[0], 1, 0))
     right = jnp.where(col == cols - 1, 0.0, pltpu.roll(parts[2], pixels - 1, 0))
     return left + parts[1] + right
 
 
+def finish(dec_in, peaks_in, dec_out, peaks_out, sem):
+    copies = [
+        pltpu.make_async_copy(dec_in, dec_out, sem.at[0]),
+        pltpu.make_async_copy(peaks_in, peaks_out, sem.at[1]),
+    ]
+    for copy in copies:
+        copy.start()
+    for copy in copies:
+        copy.wait()
+
+
 def kernel(
     R, T, lat_hbm, g1_ref, w1_hbm, g2_ref, w2_hbm, up_hbm, dec_ref, peaks_ref,
     lat, prev, first, second, w1, w2, up, merged, pk_send, pk_recv,
-    load_sem, x1_send, x1_recv, rl_send, rl_recv, s_send, s_recv, x3_send, x3_recv, pk_ssem, pk_rsem, known,
+    load_sem, x1_send, x1_recv, rl_send, rl_recv, s_send, s_recv, x3_send, x3_recv, pk_ssem, pk_rsem, known, spread,
 ):
     r = lax.axis_index("rows")
     t = lax.axis_index("tm")
@@ -109,6 +125,13 @@
     w2[:, C:, :] = jnp.zeros((w2.shape[0], pad, C), BF16)
     pk_send[...] = jnp.zeros_like(pk_send)
 
+    width = frames * cols
+    q = lax.broadcasted_iota(jnp.int32, (2 * width, 2 * width), 0)
+    o = lax.broadcasted_iota(jnp.int32, (2 * width, 2 * width), 1)
+    frame = lax.rem(lax.div(q, cols), frames)
+    target = frame * (2 * cols) + 2 * lax.rem(q, cols) + lax.div(q, width)
+    spread[...] = jnp.where(o == target, 1.0, 0.0).astype(BF16)
+
     loads[0].wait()
     rows_near = 1 + jnp.minimum(r, REACH) + jnp.minimum(R - 1 - r, REACH)
     pl.semaphore_wait(barrier, rows_near * T - 1)
@@ -180,6 +203,9 @@
         hear(i - 1)
         tell(i)
 
+    loads[1].wait()
+    parts = taps_part(first, w1, (2,), frames, 3, cols)
+
     @pl.when(takes)
     def _():
         for d in [0] + offsets:
@@ -190,8 +216,8 @@
                 relay(slot).wait_recv()
                 put_first(prev, slot, 0)
 
-    loads[1].wait()
-    hidden = taps_sum(first, w1, frames, 3, cols).astype(BF16).astype(F32)
+    more = taps_part(first, w1, (0, 1), frames, 3, cols)
+    hidden = shifted_sum(parts, more, cols).astype(BF16).astype(F32)
     activated = normed_silu(hidden, gain2).reshape(frames, 3, cols, C)
     zeros = jnp.zeros((frames, cols, C), BF16)
     for j in range(3):
@@ -209,9 +235,11 @@
     pl.when(gives)(lambda: hand_on().start())
     put_peak(1, peak_of(activated[:, 1].reshape(frames * cols, C)))
     loads[2].wait()
+    parts = taps_part(second, w2, (2,), frames, 1, cols)
     pl.when(takes)(lambda: hand_on().wait_recv())
 
-    block = lat[REACH].astype(F32).reshape(frames * cols, C) + taps_sum(second, w2, frames, 1, cols)
+    more = taps_part(second, w2, (0, 1), frames, 1, cols)
+    block = lat[REACH].astype(F32).reshape(frames * cols, C) + shifted_sum(parts, more, cols)
     block = block.astype(BF16)
     merged[1] = block.reshape(frames, cols, C)
     put_peak(2, peak_of(block))
@@ -244,7 +272,6 @@
 
     loads[3].wait()
     C2 = dec_ref.shape[2]
-    width = frames * cols
     own = dot_nt(up[...], block).reshape(3, 3, C2, width)
     upper = own[1] + own[2]
     lower = own[0] + own[1]
@@ -262,12 +289,7 @@
         return jnp.concatenate([even, odd], axis=1).astype(BF16)
 
     narrow = jnp.concatenate([columns(upper), columns(lower)], axis=0)
-    q = lax.broadcasted_iota(jnp.int32, (2 * width, 2 * width), 0)
-    o = lax.broadcasted_iota(jnp.int32, (2 * width, 2 * width), 1)
-    frame = lax.rem(lax.div(q, cols), frames)
-    target = frame * (2 * cols) + 2 * lax.rem(q, cols) + lax.div(q, width)
-    spread = jnp.where(o == target, 1.0, 0.0).astype(BF16)
-    wide = dot(narrow, spread).astype(BF16)
+    wide = dot(narrow, spread[...]).astype(BF16)
     for f in range(frames):
         for j in range(2):
             dec_ref[f, j] = wide[j * C2 : (j + 1) * C2, f * 2 * cols : (f + 1) * 2 * cols]
@@ -311,7 +333,7 @@
     vmem = pl.BlockSpec(memory_space=pltpu.VMEM)
     hbm = pl.BlockSpec(memory_space=pl.ANY)
     dma = pltpu.SemaphoreType.DMA
-    return pl.pallas_call(
+    decoded, peaks = pl.pallas_call(
         functools.partial(kernel, R, T),
         out_shape=(
             jax.ShapeDtypeStruct((frames, 2 * rows, C2, 2 * cols), BF16),
@@ -342,8 +364,9 @@
             dma((n,)),
             dma((n,)),
             pltpu.SemaphoreType.REGULAR((R.bit_length(), 2)),
+            pltpu.VMEM((2 * frames * cols, 2 * frames * cols), BF16),
         ],
-        compiler_params=pltpu.CompilerParams(collective_id=0, has_side_effects=True),
+        compiler_params=pltpu.CompilerParams(collective_id=0, has_side_effects=True, vmem_limit_bytes=54 * 2**20),
     )(
         latent.reshape(frames, cols, C),
         gain_first,
@@ -352,6 +375,16 @@
         conv_second.reshape(taps, C, C),
         conv_up.reshape(9 * C2, C),
     )
+    return pl.pallas_call(
+        finish,
+        out_shape=(
+            jax.ShapeDtypeStruct(decoded.shape, BF16),
+            jax.ShapeDtypeStruct(peaks.shape, F32),
+        ),
+        in_specs=[vmem, vmem],
+        out_specs=(hbm, hbm),
+        scratch_shapes=[dma((2,))],
+    )(decoded, peaks)
 
 
 def solution(mesh):

time: 24.4 us -> 23.3 us (0.955)
  local copies, waits for them, and re-layouts: 2.82 us -> 0 us
  Pallas kernels: 20.8 us -> 22.5 us
    unnamed x2 -> x0, local copies, waits for them, and re-layouts: 2.82 us -> none
    pallas_call x0 -> x1, Pallas kernels: none -> 1.55 us  [per_device(): pl.pallas_call(finish, out_shape=(jax.ShapeDtypeStruct(decoded.shape, BF1...]
where the time goes in v3:
time: 23.3 us; the launch traced here: 23.1 us
  Pallas kernels  22.5 us (97%)
  between operations  0.64 us (3%)
    pallas_call x1, Pallas kernels, per_device(): pl.pallas_call(functools.partial(kernel, R, T), out_shape=(jax.ShapeDtype...  21 us
    pallas_call x1, Pallas kernels, per_device(): pl.pallas_call(finish, out_shape=(jax.ShapeDtypeStruct(decoded.shape, BF1...  1.55 us

profile of v3, /device:TPU:0, one launch (start us, length us, event | category | flops | bytes accessed | tf_op | source)
XLA Modules:
  0.0 23.1 jit_solution(2479263718844163633)
XLA Ops:
  0.6 21.0 %shard_map.77 = (bf16[2,2,96,128]{3,2,1,0:T(8,128)(2,1)}, f32[3,192]{1,0:T(4,128)}) custom-call(bf16[2,64,192]{2,1,0:T(8,128)(2,1)} %bitcast.7, bf16[192]{0:T(256)(128)(2,1)} %g1_ref.1, bf16[27,192,192]{2,1,0:T(8,128)(2,1)} %bitcast.4, bf16[192]{0:T(256)(128)(2,1)} %g2_ref.1, bf16[27,192,192]{2,1,0:T(8,128)(2,1)} %bitcast.5, bf16[864,192]{1,0:T(8,128)(2,1)} %bitcast.6), custom_call_target="tpu_custom_call" | custom-call | tf_op jit(solution)/shard_map/pallas_call | solution.py:336
  21.6 1.6 %shard_map.78 = (bf16[2,2,96,128]{3,2,1,0:T(8,128)(2,1)}, f32[3,192]{1,0:T(4,128)}) custom-call(bf16[2,2,96,128]{3,2,1,0:T(8,128)(2,1)} %get-tuple-element.4.dec_in, f32[3,192]{1,0:T(4,128)} %get-tuple-element.5.peaks_in), custom_call_target="tpu_custom_call" | custom-call | tf_op jit(solution)/shard_map/pallas_call | solution.py:378
